TPU v7x, 32 devices: a whole 2x2x4 slice. The times are simulated.
32 devices in a mesh: dp: 8 (over z, core), tensor: 4 (over y, x).
Axes of the slice: x: 2, y: 2, z: 4, core: 2. Of those that a mesh axis runs over, the one named last changes fastest.
Arguments:
- inputs: bfloat16 [8192, 2048], P(('dp', 'tensor'))
- doc_lengths: int32 [8, 4], P('dp'), may hold values from 0 to 1024, as said below
- attn_gain: bfloat16 [2048], P('dp'), may hold values from 0.099609375 to 1.8984375
- w_query: bfloat16 [2048, 2048], P('dp', 'tensor')
- w_key: bfloat16 [2048, 512], P('dp', 'tensor')
- value_weight: bfloat16 [2048, 512], P('dp', 'tensor'), may hold values from -0.125 to 0.125
- w_output: bfloat16 [2048, 2048], P('tensor', 'dp'), may hold values from -0.5 to 0.5
- mlp_gain: bfloat16 [2048], P('dp'), may hold values from 0.099609375 to 1.8984375
- w_gate: bfloat16 [2048, 8192], P('dp', 'tensor'), may hold values from -0.125 to 0.125
- w_up: bfloat16 [2048, 8192], P('dp', 'tensor'), may hold values from -0.125 to 0.125
- w_down: bfloat16 [8192, 2048], P('tensor', 'dp'), may hold values from -0.125 to 0.125
- out_grad: bfloat16 [8192, 2048], P(('dp', 'tensor')), may hold values from -6 to 6
Outputs:
- output: float32 [8192, 2048], P(('dp', 'tensor'))
- input_grad: float32 [8192, 2048], P(('dp', 'tensor'))
- attn_gain_grad: float32 [2048], P('dp')
- w_query_grad: float32 [2048, 2048], P('dp', 'tensor')
- w_key_grad: float32 [2048, 512], P('dp', 'tensor')
- w_value_grad: float32 [2048, 512], P('dp', 'tensor')
- w_output_grad: float32 [2048, 2048], P('tensor', 'dp')
- mlp_gain_grad: float32 [2048], P('dp')
- w_gate_grad: float32 [2048, 8192], P('dp', 'tensor')
- w_up_grad: float32 [2048, 8192], P('dp', 'tensor')
- w_down_grad: float32 [8192, 2048], P('tensor', 'dp')
Inputs may be any that keep to these rules, and one draw needn't show every extreme that they name: `doc_lengths`: row r lists the lengths of the 4 documents packed back to back from the first slot of dp index r; a row sums to at most 1024, zero lengths occur, and in every draw some row holds a single document of 1024 tokens.
All inputs are finite; a program needn't handle non-finite values.
Results may differ from a plain program's by a relative error of at most 0.017.
The roundings to bfloat16 on the way count: a program that leaves them out, or rounds other values in their place, can miss the bound.
Values may be sent and summed in bfloat16 or wider, within the bound.
A program may use at most 256 MiB of HBM per device.

v0:
```python
import jax
import jax.numpy as jnp
from jax import lax
from jax.sharding import PartitionSpec as P

HEAD_SIZE = 64
QBLK = 512
epsilon = 1e-05
rope_base = 500000.0


def layout(lengths, total_rows):
    row_index = jnp.arange(total_rows, dtype=jnp.int32)
    doc_ends = jnp.cumsum(lengths)
    passed = doc_ends[None, :] <= row_index[:, None]
    document_segment = jnp.sum(passed.astype(jnp.int32), axis=1)
    doc_start = jnp.sum(jnp.where(passed, lengths[None, :], 0), axis=1)
    positions = (row_index - doc_start).astype(jnp.float32)
    valid_rows = (document_segment < lengths.shape[0]).astype(jnp.float32)
    return (document_segment, positions, valid_rows)


def rope_tables(positions, head_dim):
    half_dim = head_dim // 2
    inverse_freq = rope_base ** (-(jnp.arange(half_dim, dtype=jnp.float32) * 2.0 / head_dim))
    angles = positions[:, None] * inverse_freq[None, :]
    return (jnp.cos(angles)[:, None, :], jnp.sin(angles)[:, None, :])


def rotate(tensor, cosine, sine_part, direction):
    half_dim = tensor.shape[-1] // 2
    first_half = tensor[..., :half_dim]
    second_half = tensor[..., half_dim:]
    return jnp.concatenate(
        [
            first_half * cosine - direction * second_half * sine_part,
            second_half * cosine + direction * first_half * sine_part,
        ],
        axis=-1,
    )


def rms_stats(hidden):
    scale_row = lax.rsqrt(jnp.mean(hidden * hidden, axis=-1, keepdims=True) + epsilon)
    return (scale_row, hidden * scale_row)


def norm_backward(grad_normed, unit_rows, scale_row, gain_wide):
    scaled = grad_normed * gain_wide
    return scale_row * (scaled - unit_rows * jnp.mean(scaled * unit_rows, axis=-1, keepdims=True))


def block_mask(document_segment, first_row, block_rows):
    row_index = jnp.arange(document_segment.shape[0], dtype=jnp.int32)
    query_rows = first_row + jnp.arange(block_rows, dtype=jnp.int32)
    query_segment = lax.dynamic_slice_in_dim(document_segment, first_row, block_rows, 0)
    return (query_segment[:, None] == document_segment[None, :]) & (
        row_index[None, :] <= query_rows[:, None]
    )


def attention_forward(queries, keys_rot, values, document_segment, block_rows):
    total_rows, kv_heads, group_size, head_dim = queries.shape
    score_scale = head_dim ** (-0.5)

    def one_block(block_index):
        first_row = block_index * block_rows
        query_block = lax.dynamic_slice_in_dim(queries, first_row, block_rows, 0)
        allowed = block_mask(document_segment, first_row, block_rows)
        scores = (
            jnp.einsum("qkgd,skd->kgqs", query_block, keys_rot, preferred_element_type=jnp.float32)
            * score_scale
        )
        scores = jnp.where(allowed, scores, -jnp.inf)
        row_max = jnp.max(scores, axis=-1, keepdims=True)
        log_total = row_max + jnp.log(jnp.sum(jnp.exp(scores - row_max), axis=-1, keepdims=True))
        weights = jnp.exp(scores - log_total).astype(jnp.bfloat16)
        attended = jnp.einsum("kgqs,skd->qkgd", weights, values, preferred_element_type=jnp.float32)
        return (attended.astype(jnp.bfloat16), log_total[..., 0])

    attended, log_total = lax.map(one_block, jnp.arange(total_rows // block_rows, dtype=jnp.int32))
    return (attended.reshape(total_rows, kv_heads, group_size, head_dim), log_total)


def attention_backward(
    queries, keys_rot, values, attended, grad_attended, log_total, document_segment, block_rows
):
    total_rows, kv_heads, group_size, head_dim = queries.shape
    score_scale = head_dim ** (-0.5)

    def one_block(running, block_index):
        key_grad, value_grad = running
        first_row = block_index * block_rows
        query_block = lax.dynamic_slice_in_dim(queries, first_row, block_rows, 0)
        block_gradient = lax.dynamic_slice_in_dim(grad_attended, first_row, block_rows, 0)
        out_block = lax.dynamic_slice_in_dim(attended, first_row, block_rows, 0)
        allowed = block_mask(document_segment, first_row, block_rows)
        scores = (
            jnp.einsum("qkgd,skd->kgqs", query_block, keys_rot, preferred_element_type=jnp.float32)
            * score_scale
        )
        scores = jnp.where(allowed, scores, -jnp.inf)
        prob_full = jnp.exp(scores - log_total[block_index][..., None])
        weights = prob_full.astype(jnp.bfloat16)
        value_grad = value_grad + jnp.einsum(
            "kgqs,qkgd->skd", weights, block_gradient, preferred_element_type=jnp.float32
        )
        grad_probs = jnp.einsum(
            "qkgd,skd->kgqs", block_gradient, values, preferred_element_type=jnp.float32
        )
        row_delta = jnp.einsum(
            "qkgd,qkgd->kgq", block_gradient, out_block, preferred_element_type=jnp.float32
        )
        grad_scores = (prob_full * (grad_probs - row_delta[..., None])).astype(jnp.bfloat16)
        query_grad = (
            jnp.einsum("kgqs,skd->qkgd", grad_scores, keys_rot, preferred_element_type=jnp.float32)
            * score_scale
        )
        key_grad = (
            key_grad
            + jnp.einsum(
                "kgqs,qkgd->skd", grad_scores, query_block, preferred_element_type=jnp.float32
            )
            * score_scale
        )
        return ((key_grad, value_grad), query_grad)

    zero_keys = jnp.zeros((total_rows, kv_heads, head_dim), jnp.float32)
    (key_grad, value_grad), query_grad = lax.scan(
        one_block, (zero_keys, zero_keys), jnp.arange(total_rows // block_rows, dtype=jnp.int32)
    )
    return (query_grad.reshape(total_rows, kv_heads * group_size, head_dim), key_grad, value_grad)


def attn_params(attn_gain, w_query, w_key, value_weight, w_output):
    return (
        lax.all_gather(attn_gain, "dp", axis=0, tiled=True),
        lax.all_gather(w_query, "dp", axis=0, tiled=True),
        lax.all_gather(w_key, "dp", axis=0, tiled=True),
        lax.all_gather(value_weight, "dp", axis=0, tiled=True),
        lax.all_gather(w_output, "dp", axis=1, tiled=True),
    )


def mlp_params(mlp_gain, w_gate, w_up, w_down):
    return (
        lax.all_gather(mlp_gain, "dp", axis=0, tiled=True),
        lax.all_gather(w_gate, "dp", axis=0, tiled=True),
        lax.all_gather(w_up, "dp", axis=0, tiled=True),
        lax.all_gather(w_down, "dp", axis=1, tiled=True),
    )


def per_device(
    inputs,
    doc_lengths,
    attn_gain,
    w_query,
    w_key,
    value_weight,
    w_output,
    mlp_gain,
    w_gate,
    w_up,
    w_down,
    out_grad,
):
    tensor_count = lax.axis_size("tensor")
    tensor_rank = lax.axis_index("tensor")
    own_rows = inputs.shape[0]
    total_rows = own_rows * tensor_count
    document_segment, positions, valid_rows = layout(doc_lengths[0], total_rows)
    valid_own = lax.dynamic_slice_in_dim(valid_rows, tensor_rank * own_rows, own_rows, 0)[:, None]
    cosine, sine_part = rope_tables(positions, HEAD_SIZE)
    gain_one, full_query, full_key, full_value, full_output = attn_params(
        attn_gain, w_query, w_key, value_weight, w_output
    )
    gain_two, full_gate, full_up, complete_down_weight = mlp_params(mlp_gain, w_gate, w_up, w_down)
    head_count = full_query.shape[1] // HEAD_SIZE
    kv_heads = full_key.shape[1] // HEAD_SIZE
    group_size = head_count // kv_heads
    residual = inputs.astype(jnp.float32)
    scale_one, unit_one = rms_stats(residual)
    normed_one = (unit_one * gain_one.astype(jnp.float32)).astype(jnp.bfloat16)
    normed_one_all = lax.all_gather(normed_one, "tensor", axis=0, tiled=True)
    query_full = jnp.dot(normed_one_all, full_query, preferred_element_type=jnp.float32).reshape(
        total_rows, head_count, HEAD_SIZE
    )
    queries = (
        rotate(query_full, cosine, sine_part, 1.0)
        .astype(jnp.bfloat16)
        .reshape(total_rows, kv_heads, group_size, HEAD_SIZE)
    )
    key_full = jnp.dot(normed_one_all, full_key, preferred_element_type=jnp.float32).reshape(
        total_rows, kv_heads, HEAD_SIZE
    )
    keys_rot = rotate(key_full, cosine, sine_part, 1.0).astype(jnp.bfloat16)
    values = jnp.dot(normed_one_all, full_value, preferred_element_type=jnp.float32).astype(
        jnp.bfloat16
    )
    values = values.reshape(total_rows, kv_heads, HEAD_SIZE)
    attended, log_total = attention_forward(queries, keys_rot, values, document_segment, QBLK)
    attended_flat = attended.reshape(total_rows, head_count * HEAD_SIZE)
    rows_part = attended_flat
    attn_out = lax.psum_scatter(
        jnp.dot(rows_part, full_output, preferred_element_type=jnp.float32),
        "tensor",
        scatter_dimension=0,
        tiled=True,
    )
    hidden = residual + valid_own * attn_out
    scale_two, unit_two = rms_stats(hidden)
    normed_two = (unit_two * gain_two.astype(jnp.float32)).astype(jnp.bfloat16)
    normed_two_all = lax.all_gather(normed_two, "tensor", axis=0, tiled=True)
    gate_pre = jnp.dot(normed_two_all, full_gate, preferred_element_type=jnp.float32)
    up_proj = jnp.dot(normed_two_all, full_up, preferred_element_type=jnp.float32)
    sigmoid_gate = jax.nn.sigmoid(gate_pre)
    activation = (gate_pre * sigmoid_gate * up_proj).astype(jnp.bfloat16)
    rows_part = activation
    mlp_out = lax.psum_scatter(
        jnp.dot(rows_part, complete_down_weight, preferred_element_type=jnp.float32),
        "tensor",
        scatter_dimension=0,
        tiled=True,
    )
    output = hidden + valid_own * mlp_out
    gain_one, full_query, full_key, full_value, full_output = attn_params(
        attn_gain, w_query, w_key, value_weight, w_output
    )
    gain_two, full_gate, full_up, complete_down_weight = mlp_params(mlp_gain, w_gate, w_up, w_down)
    grad_out = out_grad.astype(jnp.float32)
    grad_mlp = (grad_out * valid_own).astype(jnp.bfloat16)
    grad_mlp_all = lax.all_gather(grad_mlp, "tensor", axis=0, tiled=True)
    w_down_part = jnp.dot(activation.T, grad_mlp_all, preferred_element_type=jnp.float32)
    grad_act = jnp.dot(grad_mlp_all, complete_down_weight.T, preferred_element_type=jnp.float32)
    grad_gate = (
        grad_act * up_proj * sigmoid_gate * (1.0 + gate_pre * (1.0 - sigmoid_gate))
    ).astype(jnp.bfloat16)
    grad_up = (grad_act * gate_pre * sigmoid_gate).astype(jnp.bfloat16)
    grad_normed_two = lax.psum_scatter(
        jnp.dot(grad_gate, full_gate.T, preferred_element_type=jnp.float32)
        + jnp.dot(grad_up, full_up.T, preferred_element_type=jnp.float32),
        "tensor",
        scatter_dimension=0,
        tiled=True,
    )
    w_gate_part = jnp.dot(normed_two_all.T, grad_gate, preferred_element_type=jnp.float32)
    w_up_part = jnp.dot(normed_two_all.T, grad_up, preferred_element_type=jnp.float32)
    mlp_gain_part = jnp.sum(grad_normed_two * unit_two, axis=0)
    mlp_gain_slice, w_gate_grad, w_up_grad, w_down_grad = (
        lax.psum_scatter(mlp_gain_part, "dp", scatter_dimension=0, tiled=True),
        lax.psum_scatter(w_gate_part, "dp", scatter_dimension=0, tiled=True),
        lax.psum_scatter(w_up_part, "dp", scatter_dimension=0, tiled=True),
        lax.psum_scatter(w_down_part, "dp", scatter_dimension=1, tiled=True),
    )
    grad_hidden = grad_out + norm_backward(
        grad_normed_two, unit_two, scale_two, gain_two.astype(jnp.float32)
    )
    grad_attn = (grad_hidden * valid_own).astype(jnp.bfloat16)
    grad_attn_all = lax.all_gather(grad_attn, "tensor", axis=0, tiled=True)
    w_output_part = jnp.dot(attended_flat.T, grad_attn_all, preferred_element_type=jnp.float32)
    grad_attended = jnp.dot(
        grad_attn_all, full_output.T, preferred_element_type=jnp.float32
    ).astype(jnp.bfloat16)
    grad_attended = grad_attended.reshape(total_rows, kv_heads, group_size, HEAD_SIZE)
    query_grad, key_grad, value_grad = attention_backward(
        queries, keys_rot, values, attended, grad_attended, log_total, document_segment, QBLK
    )
    query_back = (
        rotate(query_grad, cosine, sine_part, -1.0)
        .astype(jnp.bfloat16)
        .reshape(total_rows, head_count * HEAD_SIZE)
    )
    key_back = (
        rotate(key_grad, cosine, sine_part, -1.0)
        .astype(jnp.bfloat16)
        .reshape(total_rows, kv_heads * HEAD_SIZE)
    )
    value_back = value_grad.astype(jnp.bfloat16).reshape(total_rows, kv_heads * HEAD_SIZE)
    grad_normed_one = lax.psum_scatter(
        jnp.dot(query_back, full_query.T, preferred_element_type=jnp.float32)
        + jnp.dot(key_back, full_key.T, preferred_element_type=jnp.float32)
        + jnp.dot(value_back, full_value.T, preferred_element_type=jnp.float32),
        "tensor",
        scatter_dimension=0,
        tiled=True,
    )
    w_query_part = jnp.dot(normed_one_all.T, query_back, preferred_element_type=jnp.float32)
    w_key_part = jnp.dot(normed_one_all.T, key_back, preferred_element_type=jnp.float32)
    w_value_part = jnp.dot(normed_one_all.T, value_back, preferred_element_type=jnp.float32)
    attn_gain_part = jnp.sum(grad_normed_one * unit_one, axis=0)
    attn_gain_slice, w_query_grad, w_key_grad, w_value_grad, w_output_grad = (
        lax.psum_scatter(attn_gain_part, "dp", scatter_dimension=0, tiled=True),
        lax.psum_scatter(w_query_part, "dp", scatter_dimension=0, tiled=True),
        lax.psum_scatter(w_key_part, "dp", scatter_dimension=0, tiled=True),
        lax.psum_scatter(w_value_part, "dp", scatter_dimension=0, tiled=True),
        lax.psum_scatter(w_output_part, "dp", scatter_dimension=1, tiled=True),
    )
    input_grad = grad_hidden + norm_backward(
        grad_normed_one, unit_one, scale_one, gain_one.astype(jnp.float32)
    )
    gain_sums = lax.psum((attn_gain_slice, mlp_gain_slice), "tensor")
    return (
        output,
        input_grad,
        gain_sums[0],
        w_query_grad,
        w_key_grad,
        w_value_grad,
        w_output_grad,
        gain_sums[1],
        w_gate_grad,
        w_up_grad,
        w_down_grad,
    )


def solution(mesh):
    placed = (
        P(("dp", "tensor"), None),
        P("dp", None),
        P("dp"),
        P("dp", "tensor"),
        P("dp", "tensor"),
        P("dp", "tensor"),
        P("tensor", "dp"),
        P("dp"),
        P("dp", "tensor"),
        P("dp", "tensor"),
        P("tensor", "dp"),
        P(("dp", "tensor"), None),
    )
    return jax.shard_map(
        per_device,
        mesh=mesh,
        in_specs=placed,
        out_specs=(
            P(("dp", "tensor"), None),
            P(("dp", "tensor"), None),
            P("dp"),
            P("dp", "tensor"),
            P("dp", "tensor"),
            P("dp", "tensor"),
            P("tensor", "dp"),
            P("dp"),
            P("dp", "tensor"),
            P("dp", "tensor"),
            P("tensor", "dp"),
        ),
        check_vma=False,
    )
```

profile of v0, /device:TPU:0, one launch (start us, length us, event | category | flops | bytes accessed | tf_op | source)
XLA Modules:
  0.0 1804.1 jit_solution(7006812651238048975)
XLA Ops:
  27.9 17.3 all_gather.51
  61.3 38.9 %all-gather.12.cloned.1.call-done = bf16[1024,2048]{1,0:T(8,128)(2,1)} async-done(((bf16[256,2048]{1,0:T(8,128)(2,1)}), bf16[1024,2048]{1,0:T(8,128)(2,1)}) %all-gather.12.cloned.1.call-update) | async-done | bytes 4194320 | tf_op jit(solution)/shard_map/all_gather | solution.py:185
  109.2 27.3 %while.27 = (s32[]{:T(128)}, bf16[2,512,2,4,64]{1,4,3,2,0:T(8,128)(2,1)S(1)}, f32[2,2,4,512]{3,2,1,0:T(4,128)S(1)}, s32[2]{0:T(128)S(1)}, s32[1024]{0:T(1024)S(1...) while((s32[]{:T(128)}, ...), condition=%wide.region_7.8_spmd, body=%wide.region_4.7_spmd.sunk | while | flops 1121710592 | bytes 54147264 | solution.py:81
  159.0 74.0 %reduce-scatter.12.cloned.1.call-done = f32[256,2048]{1,0:T(8,128)} async-done(((f32[1024,2048]{1,0:T(8,128)}), f32[256,2048]{1,0:T(8,128)}) %reduce-scatter.12.cloned.1.call-update) | async-done | bytes 2097168 | tf_op jit(solution)/shard_map/reduce_scatter | solution.py:205
  240.6 75.9 %all-gather.20.cloned.1.call-done = bf16[2048,2048]{1,0:T(8,128)(2,1)} async-done(((bf16[256,2048]{1,0:T(8,128)(2,1)}), bf16[2048,2048]{1,0:T(8,128)(2,1)}) %all-gather.20.cloned.1.call-update) | async-done | bytes 8388624 | tf_op jit(solution)/shard_map/all_gather | solution.py:148
  316.5 53.4 %all-gather.18.cloned.1.call-done = bf16[1024,2048]{1,0:T(8,128)(2,1)} async-done(((bf16[256,2048]{1,0:T(8,128)(2,1)}), bf16[1024,2048]{1,0:T(8,128)(2,1)}) %all-gather.18.cloned.1.call-update) | async-done | bytes 4194320 | tf_op jit(solution)/shard_map/all_gather | solution.py:214
  384.6 68.9 %all-gather.22.cloned.1.call-done = bf16[2048,2048]{1,0:T(8,128)(2,1)} async-done(((bf16[256,2048]{1,0:T(8,128)(2,1)}), bf16[2048,2048]{1,0:T(8,128)(2,1)}) %all-gather.22.cloned.1.call-update) | async-done | bytes 8388624 | tf_op jit(solution)/shard_map/all_gather | solution.py:149
  467.9 68.2 %all-gather.24.cloned.1.call-done = bf16[2048,2048]{1,0:T(8,128)(2,1)} async-done(((bf16[2048,256]{1,0:T(8,128)(2,1)}), bf16[2048,2048]{1,0:T(8,128)(2,1)}) %all-gather.24.cloned.1.call-update) | async-done | bytes 8388624 | tf_op jit(solution)/shard_map/all_gather | solution.py:150
  536.1 53.2 %all-gather.26.cloned.1.call-done = bf16[1024,2048]{1,0:T(8,128)(2,1)} async-done(((bf16[256,2048]{1,0:T(8,128)(2,1)}), bf16[1024,2048]{1,0:T(8,128)(2,1)}) %all-gather.26.cloned.1.call-update) | async-done | bytes 4194320 | tf_op jit(solution)/shard_map/all_gather | solution.py:233
  589.3 22.0 %multiply_convert_fusion = (bf16[1024,2048]{1,0:T(8,128)(2,1)}, bf16[1024,2048]{1,0:T(8,128)(2,1)}, bf16[1024,2048]{1,0:T(8,128)(2,1)}) fusion(f32[1024,2048]{1,0:T(8,128)} %fusion.71, f32[1024,2048]{1,0:T(8,128)} %fusion.72, bf16[1024,2048]{1,0:T(8,128)(2,1)} %all-gather.26.cloned.1.call-done, bf16[2048,2048]{1,0:T(8,128)(2,1)} %all-gather.24.cloned.1.call-done), kind=kOutput, calls=%fused_computation.62 | convolution fusion | flops 8623489024 | bytes 41943040 | tf_op jit(solution)/shard_map/dot_general | solution.py:235
  653.6 71.9 %reduce-scatter.16.cloned.1.call-done = f32[256,2048]{1,0:T(8,128)} async-done(((f32[1024,2048]{1,0:T(8,128)}), f32[256,2048]{1,0:T(8,128)}) %reduce-scatter.16.cloned.1.call-update) | async-done | bytes 2097168 | tf_op jit(solution)/shard_map/reduce_scatter | solution.py:240
  728.3 86.7 %reduce-scatter.14.cloned.1.call-done = f32[256,2048]{1,0:T(8,128)} async-done(((f32[1024,2048]{1,0:T(8,128)}), f32[256,2048]{1,0:T(8,128)}) %reduce-scatter.14.cloned.1.call-update) | async-done | bytes 2097168 | tf_op jit(solution)/shard_map/reduce_scatter | solution.py:220
  824.4 48.4 %all-gather.28.cloned.1.call-done = bf16[1024,2048]{1,0:T(8,128)(2,1)} async-done(((bf16[256,2048]{1,0:T(8,128)(2,1)}), bf16[1024,2048]{1,0:T(8,128)(2,1)}) %all-gather.28.cloned.1.call-update) | async-done | bytes 4194320 | tf_op jit(solution)/shard_map/all_gather | solution.py:260
  878.3 132.7 %while.28 = (s32[]{:T(128)}, f32[1024,2,64]{0,2,1:T(8,128)}, f32[1024,2,64]{0,2,1:T(8,128)}, f32[2,512,2,4,64]{1,0,4,3,2:T(2,128)}, s32[2]{0:T(128)S(1)}, /*inde...) while((s32[]{:T(128)}, f32[1024,2,64]{0,2,1:T(8,128)}, ...), condition=%wide.region_14.15_spmd.clone, body=%wide.region_13.14_spmd.clone.sunk | while | flops 2729832960 | bytes 146422416 | solution.py:129
  910.9 19.6 %dynamic_update_slice.20 = f32[2,512,2,4,64]{1,0,4,3,2:T(2,128)} dynamic-update-slice(f32[2,512,2,4,64]{1,0,4,3,2:T(2,128)} %get-tuple-element.421, f32[1,512,2,4,64]{1,0,4,3,2:T(1,128)S(1)} %copy.60, s32[]{:T(128)} %get-tuple-element.418, s32[]{:T(128)} %constant.45.clone.1..sunk.1, s32[]{:T(128)} %constant.45.clone.1..sunk.1, s32[]{:T(128)} %constant.45.clone.1..sunk.1, s32[]{:T(128)} %constant.45.clone.1..sunk.1) | dynamic-update-slice | bytes 2097156 | tf_op jit(solution)/shard_map/while/body/jit(dynamic_update_index_in_dim)/dynamic_update_slice | solution.py:129
  976.9 19.6 %dynamic_update_slice.20 = f32[2,512,2,4,64]{1,0,4,3,2:T(2,128)} dynamic-update-slice(f32[2,512,2,4,64]{1,0,4,3,2:T(2,128)} %get-tuple-element.421, f32[1,512,2,4,64]{1,0,4,3,2:T(1,128)S(1)} %copy.60, s32[]{:T(128)} %get-tuple-element.418, s32[]{:T(128)} %constant.45.clone.1..sunk.1, s32[]{:T(128)} %constant.45.clone.1..sunk.1, s32[]{:T(128)} %constant.45.clone.1..sunk.1, s32[]{:T(128)} %constant.45.clone.1..sunk.1) | dynamic-update-slice | bytes 2097156 | tf_op jit(solution)/shard_map/while/body/jit(dynamic_update_index_in_dim)/dynamic_update_slice | solution.py:129
  1070.5 15.5 fusion.82
  1119.8 28.5 %all-reduce.2 = (f32[2048]{0:T(1024)S(1)}, f32[2048]{0:T(1024)S(1)}) all-reduce(f32[2048]{0:T(1024)S(1)} %get-tuple-element.164, f32[2048]{0:T(1024)S(1)} %copy-done.33), channel_id=6, replica_groups=mesh['dp'=8,'tensor'=4] {'dp'}, use_global_device_ids=true, to_apply=%region_18.19.clone | all-reduce | flops 4096 | bytes 32768
  1163.0 23.4 %reduce-scatter.24.cloned.1.call-done = f32[256,128]{1,0:T(8,128)} async-done(((f32[2048,128]{1,0:T(8,128)}), f32[256,128]{1,0:T(8,128)}) %reduce-scatter.24.cloned.1.call-update) | async-done | bytes 131088 | tf_op jit(solution)/shard_map/reduce_scatter | solution.py:296
  1186.4 50.8 %reduce-scatter.20.cloned.1.call-done = f32[256,512]{1,0:T(8,128)} async-done(((f32[2048,512]{1,0:T(8,128)}), f32[256,512]{1,0:T(8,128)}) %reduce-scatter.20.cloned.1.call-update) | async-done | bytes 524304 | tf_op jit(solution)/shard_map/reduce_scatter | solution.py:294
  1237.3 51.1 %reduce-scatter.26.cloned.1.call-done = f32[512,256]{1,0:T(8,128)} async-done(((f32[512,2048]{1,0:T(8,128)}), f32[512,256]{1,0:T(8,128)}) %reduce-scatter.26.cloned.1.call-update) | async-done | bytes 524304 | tf_op jit(solution)/shard_map/reduce_scatter | solution.py:297
  1288.4 169.5 %reduce-scatter.28.cloned.1.call-done = f32[256,2048]{1,0:T(8,128)} async-done(((f32[2048,2048]{1,0:T(8,128)}), f32[256,2048]{1,0:T(8,128)}) %reduce-scatter.28.cloned.1.call-update) | async-done | bytes 2097168 | tf_op jit(solution)/shard_map/reduce_scatter | solution.py:252
  1457.8 169.6 %reduce-scatter.30.cloned.1.call-done = f32[256,2048]{1,0:T(8,128)} async-done(((f32[2048,2048]{1,0:T(8,128)}), f32[256,2048]{1,0:T(8,128)}) %reduce-scatter.30.cloned.1.call-update) | async-done | bytes 2097168 | tf_op jit(solution)/shard_map/reduce_scatter | solution.py:253
  1627.4 169.4 %reduce-scatter.32.cloned.1.call-done = f32[2048,256]{1,0:T(8,128)} async-done(((f32[2048,2048]{1,0:T(8,128)}), f32[2048,256]{1,0:T(8,128)}) %reduce-scatter.32.cloned.1.call-update) | async-done | bytes 2097168 | tf_op jit(solution)/shard_map/reduce_scatter | solution.py:254
  (282 shorter events, 384.4 us)
Async XLA Ops:
  7.2 54.1 %all-gather.14.cloned.1.call-start = ((), (), s32[]{:S(2)}) async-start(), calls=%async_computation.12 | async-start | bytes 2359296 | tf_op jit(solution)/shard_map/all_gather | solution.py:138
  7.9 92.2 %all-gather.12.cloned.1.call-start = ((), (), s32[]{:S(2)}) async-start(), calls=%async_computation.11 | async-start | bytes 5242880 | tf_op jit(solution)/shard_map/all_gather | solution.py:185
  26.8 112.1 %all-gather.16.cloned.1.call-start = ((), (), s32[]{:S(2)}) async-start(), calls=%async_computation.13 | async-start | bytes 2359296 | tf_op jit(solution)/shard_map/all_gather | solution.py:141
  27.5 205.4 %reduce-scatter.12.cloned.1.call-start = ((), (), s32[]{:S(2)}) async-start(), calls=%async_computation.14 | async-start | bytes 10485760 | tf_op jit(solution)/shard_map/reduce_scatter | solution.py:205
  146.5 170.0 %all-gather.20.cloned.1.call-start = ((), (), s32[]{:S(2)}) async-start(), calls=%async_computation.16 | async-start | bytes 9437184 | tf_op jit(solution)/shard_map/all_gather | solution.py:148
  147.1 222.8 %all-gather.18.cloned.1.call-start = ((), (), s32[]{:S(2)}) async-start(), calls=%async_computation.15 | async-start | bytes 5242880 | tf_op jit(solution)/shard_map/all_gather | solution.py:214
  158.9 656.1 %copy-start.27 = (f32[8,1,256]{2,1,0:T(1,128)}, f32[8,1,256]{2,1,0:T(1,128)S(1)}, u32[]{:S(2)}) copy-start(f32[8,1,256]{2,1,0:T(1,128)S(1)} %convert_element_type.105) | copy-start | bytes 24580
  236.7 578.2 %copy-start.8 = (f32[256,2048]{1,0:T(8,128)}, f32[256,2048]{1,0:T(8,128)S(1)}, u32[]{:S(2)}) copy-start(f32[256,2048]{1,0:T(8,128)S(1)} %get-tuple-element.215) | copy-start | bytes 6291460
  236.7 578.2 %copy-start.34 = (f32[256]{0:T(256)}, f32[256]{0:T(256)S(1)}, u32[]{:S(2)}) copy-start(f32[256]{0:T(256)S(1)} %add_rsqrt_fusion) | copy-start | bytes 3076
  238.3 215.2 %all-gather.22.cloned.1.call-start = ((), (), s32[]{:S(2)}) async-start(), calls=%async_computation.17 | async-start | bytes 9437184 | tf_op jit(solution)/shard_map/all_gather | solution.py:149
  239.0 297.0 %all-gather.24.cloned.1.call-start = ((), (), s32[]{:S(2)}) async-start(), calls=%async_computation.18 | async-start | bytes 9437184 | tf_op jit(solution)/shard_map/all_gather | solution.py:150
  239.8 349.5 %all-gather.26.cloned.1.call-start = ((), (), s32[]{:S(2)}) async-start(), calls=%async_computation.20 | async-start | bytes 5242880 | tf_op jit(solution)/shard_map/all_gather | solution.py:233
  240.5 485.0 %reduce-scatter.16.cloned.1.call-start = ((), (), s32[]{:S(2)}) async-start(), calls=%async_computation.21 | async-start | bytes 10485760 | tf_op jit(solution)/shard_map/reduce_scatter | solution.py:240
  639.0 175.9 %reduce-scatter.14.cloned.1.call-start = ((), (), s32[]{:S(2)}) async-start(), calls=%async_computation.19 | async-start | bytes 10485760 | tf_op jit(solution)/shard_map/reduce_scatter | solution.py:220
  653.6 219.2 %all-gather.28.cloned.1.call-start = ((), (), s32[]{:S(2)}) async-start(), calls=%async_computation.22 | async-start | bytes 5242880 | tf_op jit(solution)/shard_map/all_gather | solution.py:260
  820.1 297.5 %reduce-scatter.18.cloned.1.call-start = ((), (), s32[]{:S(2)}) async-start(), calls=%async_computation.23 | async-start | bytes 10485760 | tf_op jit(solution)/shard_map/reduce_scatter | solution.py:280
  878.3 132.7 %copy-start.17 = (f32[1024,32]{0,1:T(8,128)S(1)}, f32[1024,32]{0,1:T(8,128)}, u32[]{:S(2)}) copy-start(f32[1024,32]{0,1:T(8,128)} %copy-done.16) | copy-start | bytes 393220
  1031.1 131.9 %reduce-scatter.22.cloned.1.call-start = ((), (), s32[]{:S(2)}) async-start(), calls=%async_computation.25 | async-start | bytes 1179648 | tf_op jit(solution)/shard_map/reduce_scatter | solution.py:295
  1035.6 150.8 %reduce-scatter.24.cloned.1.call-start = ((), (), s32[]{:S(2)}) async-start(), calls=%async_computation.26 | async-start | bytes 1179648 | tf_op jit(solution)/shard_map/reduce_scatter | solution.py:296
  1040.3 197.0 %reduce-scatter.20.cloned.1.call-start = ((), (), s32[]{:S(2)}) async-start(), calls=%async_computation.24 | async-start | bytes 4718592 | tf_op jit(solution)/shard_map/reduce_scatter | solution.py:294
  1047.0 241.3 %reduce-scatter.26.cloned.1.call-start = ((), (), s32[]{:S(2)}) async-start(), calls=%async_computation.27 | async-start | bytes 4718592 | tf_op jit(solution)/shard_map/reduce_scatter | solution.py:297
  1055.0 402.9 %reduce-scatter.28.cloned.1.call-start = ((), (), s32[]{:S(2)}) async-start(), calls=%async_computation.28 | async-start | bytes 18874368 | tf_op jit(solution)/shard_map/reduce_scatter | solution.py:252
  1070.4 557.0 %reduce-scatter.30.cloned.1.call-start = ((), (), s32[]{:S(2)}) async-start(), calls=%async_computation.29 | async-start | bytes 18874368 | tf_op jit(solution)/shard_map/reduce_scatter | solution.py:253
  1086.0 710.9 %reduce-scatter.32.cloned.1.call-start = ((), (), s32[]{:S(2)}) async-start(), calls=%async_computation.30 | async-start | bytes 18874368 | tf_op jit(solution)/shard_map/reduce_scatter | solution.py:254
  (57 other events, 1034.8 us)
Sparse Core Ops, SparseCore 0:
  9.6 36.1 all-gather.13
  48.3 51.8 all-gather.11
  101.7 30.5 all-gather.15
  146.6 86.3 reduce-scatter.11
  234.4 82.0 all-gather.19
  318.7 51.0 all-gather.17
  371.4 82.0 all-gather.21
  455.1 80.9 all-gather.23
  538.5 50.7 all-gather.25
  639.2 86.3 reduce-scatter.15
  728.6 86.3 reduce-scatter.13
  820.2 52.5 all-gather.27
  1031.2 86.3 reduce-scatter.17
  1120.2 32.5 reduce-scatter.21
  1155.6 30.8 reduce-scatter.23
  1189.1 48.0 reduce-scatter.19
  1240.0 48.3 reduce-scatter.25
  1291.2 166.6 reduce-scatter.27
  1460.8 166.6 reduce-scatter.29
  1630.2 166.6 reduce-scatter.31
where the time goes:
time: 1810 us; the launch traced here: 1800 us
  waiting for transfers between devices  1290 us (71%)
  matrix products  281 us (16%)
  blocking collectives  95.4 us (5%)
  local copies, waits for them, and re-layouts  61.6 us (3%)
  other arithmetic  49.3 us (3%)
    reduce_scatter x1, waiting for transfers between devices, per_device(): lax.psum_scatter(w_up_part, 'dp', scatter_dimension=0, tiled=True)  170 us
    reduce_scatter x1, waiting for transfers between devices, per_device(): lax.psum_scatter(w_gate_part, 'dp', scatter_dimension=0, tiled=True)  169 us
    reduce_scatter x1, waiting for transfers between devices, per_device(): lax.psum_scatter(w_down_part, 'dp', scatter_dimension=1, tiled=True)  169 us
    reduce_scatter x1, waiting for transfers between devices, per_device(): lax.psum_scatter(jnp.dot(rows_part, complete_down_weight, preferred_eleme...  86.7 us
    all_gather x1, waiting for transfers between devices, mlp_params(): lax.all_gather(w_gate, 'dp', axis=0, tiled=True)  75.9 us
    reduce_scatter x1, waiting for transfers between devices, per_device(): lax.psum_scatter(jnp.dot(rows_part, full_output, preferred_element_type=j...  74 us
    reduce_scatter x1, waiting for transfers between devices, per_device(): lax.psum_scatter(jnp.dot(grad_gate, full_gate.T, preferred_element_type=j...  71.9 us
    all_gather x1, waiting for transfers between devices, mlp_params(): lax.all_gather(w_up, 'dp', axis=0, tiled=True)  68.9 us
  transfers between devices with their start and end apart: 20, of which 17 were waited for; matrix products, arithmetic and copies ran while one was open for 10% of the time, Pallas kernels for 0%

commit v1 on v0

--- a/solution.py
+++ b/solution.py
@@ -2,11 +2,22 @@
 import jax.numpy as jnp
 from jax import lax
 from jax.sharding import PartitionSpec as P
+from jax.lax import all_to_all, psum
 
 HEAD_SIZE = 64
 QBLK = 512
 epsilon = 1e-05
 rope_base = 500000.0
+
+
+def vectors_begin(xin):
+    next_value = all_to_all(
+        jnp.stack(psum(1, axis_name="tensor") * [xin], 0),
+        axis_name="tensor",
+        split_axis=0,
+        concat_axis=0,
+    )
+    return jnp.concatenate(next_value, 0)
 
 
 def layout(lengths, total_rows):
@@ -211,7 +222,7 @@
     hidden = residual + valid_own * attn_out
     scale_two, unit_two = rms_stats(hidden)
     normed_two = (unit_two * gain_two.astype(jnp.float32)).astype(jnp.bfloat16)
-    normed_two_all = lax.all_gather(normed_two, "tensor", axis=0, tiled=True)
+    normed_two_all = vectors_begin(normed_two)
     gate_pre = jnp.dot(normed_two_all, full_gate, preferred_element_type=jnp.float32)
     up_proj = jnp.dot(normed_two_all, full_up, preferred_element_type=jnp.float32)
     sigmoid_gate = jax.nn.sigmoid(gate_pre)

time: 1810 us -> 1760 us (0.972)
  waiting for transfers between devices: 1290 us -> 1230 us
    all_gather x1 -> x0, waiting for transfers between devices: 53.4 us -> none  [per_device(): normed_two_all = lax.all_gather(normed_two, 'tensor', axis=0, tiled=True)]
  transfers between devices with their start and end apart: 20 -> 20, of which waited for: 17 -> 16; matrix products, arithmetic and copies ran while one was open for 10% -> 10% of each run, Pallas kernels for 0% -> 0%
where the time goes in v1:
time: 1760 us; the launch traced here: 1750 us
  waiting for transfers between devices  1230 us (70%)
  matrix products  278 us (16%)
  blocking collectives  95.5 us (5%)
  local copies, waits for them, and re-layouts  66.2 us (4%)
  other arithmetic  47.2 us (3%)
    reduce_scatter x1, waiting for transfers between devices, per_device(): lax.psum_scatter(w_down_part, 'dp', scatter_dimension=1, tiled=True)  170 us
    reduce_scatter x1, waiting for transfers between devices, per_device(): lax.psum_scatter(w_up_part, 'dp', scatter_dimension=0, tiled=True)  169 us
    reduce_scatter x1, waiting for transfers between devices, per_device(): lax.psum_scatter(w_gate_part, 'dp', scatter_dimension=0, tiled=True)  169 us
    reduce_scatter x1, waiting for transfers between devices, per_device(): lax.psum_scatter(jnp.dot(rows_part, complete_down_weight, preferred_eleme...  86.5 us
    reduce_scatter x1, waiting for transfers between devices, per_device(): lax.psum_scatter(jnp.dot(rows_part, full_output, preferred_element_type=j...  72.7 us
    reduce_scatter x1, waiting for transfers between devices, per_device(): lax.psum_scatter(jnp.dot(grad_gate, full_gate.T, preferred_element_type=j...  71.9 us
    all_gather x1, waiting for transfers between devices, mlp_params(): lax.all_gather(w_gate, 'dp', axis=0, tiled=True)  71.4 us
    all_gather x1, waiting for transfers between devices, mlp_params(): lax.all_gather(w_down, 'dp', axis=1, tiled=True)  68.1 us
  transfers between devices with their start and end apart: 20, of which 16 were waited for; matrix products, arithmetic and copies ran while one was open for 10% of the time, Pallas kernels for 0%

profile of v1, /device:TPU:0, one launch (start us, length us, event | category | flops | bytes accessed | tf_op | source)
XLA Modules:
  0.0 1747.6 jit_solution(6626544312912468454)
XLA Ops:
  27.9 17.3 all_gather.48
  61.3 38.9 %all-gather.11.cloned.1.call-done = bf16[1024,2048]{1,0:T(8,128)(2,1)} async-done(((bf16[256,2048]{1,0:T(8,128)(2,1)}), bf16[1024,2048]{1,0:T(8,128)(2,1)}) %all-gather.11.cloned.1.call-update) | async-done | bytes 4194320 | tf_op jit(solution)/shard_map/all_gather | solution.py:196
  109.2 27.3 %while.27 = (s32[]{:T(128)}, bf16[2,512,2,4,64]{1,4,3,2,0:T(8,128)(2,1)S(1)}, f32[2,2,4,512]{3,2,1,0:T(4,128)S(1)}, s32[2]{0:T(128)S(1)}, s32[1024]{0:T(1024)S(1...) while((s32[]{:T(128)}, ...), condition=%wide.region_7.8_spmd, body=%wide.region_4.7_spmd.sunk | while | flops 1121710592 | bytes 54147264 | solution.py:92
  160.3 72.7 %reduce-scatter.12.cloned.1.call-done = f32[256,2048]{1,0:T(8,128)} async-done(((f32[1024,2048]{1,0:T(8,128)}), f32[256,2048]{1,0:T(8,128)}) %reduce-scatter.12.cloned.1.call-update) | async-done | bytes 2097168 | tf_op jit(solution)/shard_map/reduce_scatter | solution.py:216
  245.2 71.4 %all-gather.17.cloned.1.call-done = bf16[2048,2048]{1,0:T(8,128)(2,1)} async-done(((bf16[256,2048]{1,0:T(8,128)(2,1)}), bf16[2048,2048]{1,0:T(8,128)(2,1)}) %all-gather.17.cloned.1.call-update) | async-done | bytes 8388624 | tf_op jit(solution)/shard_map/all_gather | solution.py:159
  331.3 67.2 %all-gather.19.cloned.1.call-done = bf16[2048,2048]{1,0:T(8,128)(2,1)} async-done(((bf16[256,2048]{1,0:T(8,128)(2,1)}), bf16[2048,2048]{1,0:T(8,128)(2,1)}) %all-gather.19.cloned.1.call-update) | async-done | bytes 8388624 | tf_op jit(solution)/shard_map/all_gather | solution.py:160
  413.0 68.1 %all-gather.21.cloned.1.call-done = bf16[2048,2048]{1,0:T(8,128)(2,1)} async-done(((bf16[2048,256]{1,0:T(8,128)(2,1)}), bf16[2048,2048]{1,0:T(8,128)(2,1)}) %all-gather.21.cloned.1.call-update) | async-done | bytes 8388624 | tf_op jit(solution)/shard_map/all_gather | solution.py:161
  481.1 53.2 %all-gather.23.cloned.1.call-done = bf16[1024,2048]{1,0:T(8,128)(2,1)} async-done(((bf16[256,2048]{1,0:T(8,128)(2,1)}), bf16[1024,2048]{1,0:T(8,128)(2,1)}) %all-gather.23.cloned.1.call-update) | async-done | bytes 4194320 | tf_op jit(solution)/shard_map/all_gather | solution.py:244
  534.3 22.0 %multiply_convert_fusion = (bf16[1024,2048]{1,0:T(8,128)(2,1)}, bf16[1024,2048]{1,0:T(8,128)(2,1)}, bf16[1024,2048]{1,0:T(8,128)(2,1)}) fusion(f32[1024,2048]{1,0:T(8,128)} %fusion.71, f32[1024,2048]{1,0:T(8,128)} %fusion.72, bf16[1024,2048]{1,0:T(8,128)(2,1)} %all-gather.23.cloned.1.call-done, bf16[2048,2048]{1,0:T(8,128)(2,1)} %all-gather.21.cloned.1.call-done), kind=kOutput, calls=%fused_computation.62 | convolution fusion | flops 8623489024 | bytes 41943040 | tf_op jit(solution)/shard_map/dot_general | solution.py:246
  598.7 71.9 %reduce-scatter.16.cloned.1.call-done = f32[256,2048]{1,0:T(8,128)} async-done(((f32[1024,2048]{1,0:T(8,128)}), f32[256,2048]{1,0:T(8,128)}) %reduce-scatter.16.cloned.1.call-update) | async-done | bytes 2097168 | tf_op jit(solution)/shard_map/reduce_scatter | solution.py:251
  673.3 86.5 %reduce-scatter.14.cloned.1.call-done = f32[256,2048]{1,0:T(8,128)} async-done(((f32[1024,2048]{1,0:T(8,128)}), f32[256,2048]{1,0:T(8,128)}) %reduce-scatter.14.cloned.1.call-update) | async-done | bytes 2097168 | tf_op jit(solution)/shard_map/reduce_scatter | solution.py:231
  768.8 48.6 %all-gather.25.cloned.1.call-done = bf16[1024,2048]{1,0:T(8,128)(2,1)} async-done(((bf16[256,2048]{1,0:T(8,128)(2,1)}), bf16[1024,2048]{1,0:T(8,128)(2,1)}) %all-gather.25.cloned.1.call-update) | async-done | bytes 4194320 | tf_op jit(solution)/shard_map/all_gather | solution.py:271
  822.7 131.8 %while.28 = (s32[]{:T(128)}, f32[1024,2,64]{0,2,1:T(8,128)}, f32[1024,2,64]{0,2,1:T(8,128)}, f32[2,512,2,4,64]{1,0,4,3,2:T(2,128)}, s32[2]{0:T(128)S(1)}, /*inde...) while((s32[]{:T(128)}, f32[1024,2,64]{0,2,1:T(8,128)}, ...), condition=%wide.region_14.15_spmd.clone, body=%wide.region_13.14_spmd.clone.sunk | while | flops 2729832960 | bytes 148519536 | solution.py:140
  854.9 19.6 %dynamic_update_slice.20 = f32[2,512,2,4,64]{1,0,4,3,2:T(2,128)} dynamic-update-slice(f32[2,512,2,4,64]{1,0,4,3,2:T(2,128)} %get-tuple-element.421, f32[1,512,2,4,64]{1,0,4,3,2:T(1,128)S(1)} %copy.60, s32[]{:T(128)} %get-tuple-element.418, s32[]{:T(128)} %constant.45.clone.1..sunk.1, s32[]{:T(128)} %constant.45.clone.1..sunk.1, s32[]{:T(128)} %constant.45.clone.1..sunk.1, s32[]{:T(128)} %constant.45.clone.1..sunk.1) | dynamic-update-slice | bytes 2097156 | tf_op jit(solution)/shard_map/while/body/jit(dynamic_update_index_in_dim)/dynamic_update_slice | solution.py:140
  920.5 19.6 %dynamic_update_slice.20 = f32[2,512,2,4,64]{1,0,4,3,2:T(2,128)} dynamic-update-slice(f32[2,512,2,4,64]{1,0,4,3,2:T(2,128)} %get-tuple-element.421, f32[1,512,2,4,64]{1,0,4,3,2:T(1,128)S(1)} %copy.60, s32[]{:T(128)} %get-tuple-element.418, s32[]{:T(128)} %constant.45.clone.1..sunk.1, s32[]{:T(128)} %constant.45.clone.1..sunk.1, s32[]{:T(128)} %constant.45.clone.1..sunk.1, s32[]{:T(128)} %constant.45.clone.1..sunk.1) | dynamic-update-slice | bytes 2097156 | tf_op jit(solution)/shard_map/while/body/jit(dynamic_update_index_in_dim)/dynamic_update_slice | solution.py:140
  998.5 15.4 fusion.81
  1014.0 15.5 fusion.82
  1063.2 28.6 %all-reduce.2 = (f32[2048]{0:T(1024)S(1)}, f32[2048]{0:T(1024)S(1)}) all-reduce(f32[2048]{0:T(1024)S(1)} %get-tuple-element.164, f32[2048]{0:T(1024)S(1)} %copy-done.37), channel_id=6, replica_groups=mesh['dp'=8,'tensor'=4] {'dp'}, use_global_device_ids=true, to_apply=%region_18.19.clone | all-reduce | flops 4096 | bytes 32768
  1106.6 23.6 %reduce-scatter.24.cloned.1.call-done = f32[256,128]{1,0:T(8,128)} async-done(((f32[2048,128]{1,0:T(8,128)}), f32[256,128]{1,0:T(8,128)}) %reduce-scatter.24.cloned.1.call-update) | async-done | bytes 131088 | tf_op jit(solution)/shard_map/reduce_scatter | solution.py:307
  1130.1 50.9 %reduce-scatter.20.cloned.1.call-done = f32[256,512]{1,0:T(8,128)} async-done(((f32[2048,512]{1,0:T(8,128)}), f32[256,512]{1,0:T(8,128)}) %reduce-scatter.20.cloned.1.call-update) | async-done | bytes 524304 | tf_op jit(solution)/shard_map/reduce_scatter | solution.py:305
  1181.1 51.1 %reduce-scatter.26.cloned.1.call-done = f32[512,256]{1,0:T(8,128)} async-done(((f32[512,2048]{1,0:T(8,128)}), f32[512,256]{1,0:T(8,128)}) %reduce-scatter.26.cloned.1.call-update) | async-done | bytes 524304 | tf_op jit(solution)/shard_map/reduce_scatter | solution.py:308
  1232.2 169.4 %reduce-scatter.28.cloned.1.call-done = f32[256,2048]{1,0:T(8,128)} async-done(((f32[2048,2048]{1,0:T(8,128)}), f32[256,2048]{1,0:T(8,128)}) %reduce-scatter.28.cloned.1.call-update) | async-done | bytes 2097168 | tf_op jit(solution)/shard_map/reduce_scatter | solution.py:263
  1401.6 169.4 %reduce-scatter.30.cloned.1.call-done = f32[256,2048]{1,0:T(8,128)} async-done(((f32[2048,2048]{1,0:T(8,128)}), f32[256,2048]{1,0:T(8,128)}) %reduce-scatter.30.cloned.1.call-update) | async-done | bytes 2097168 | tf_op jit(solution)/shard_map/reduce_scatter | solution.py:264
  1571.1 169.6 %reduce-scatter.32.cloned.1.call-done = f32[2048,256]{1,0:T(8,128)} async-done(((f32[2048,2048]{1,0:T(8,128)}), f32[2048,256]{1,0:T(8,128)}) %reduce-scatter.32.cloned.1.call-update) | async-done | bytes 2097168 | tf_op jit(solution)/shard_map/reduce_scatter | solution.py:265
  (286 shorter events, 373.3 us)
Async XLA Ops:
  7.2 54.1 %all-gather.13.cloned.1.call-start = ((), (), s32[]{:S(2)}) async-start(), calls=%async_computation.13 | async-start | bytes 2359296 | tf_op jit(solution)/shard_map/all_gather | solution.py:149
  7.9 92.2 %all-gather.11.cloned.1.call-start = ((), (), s32[]{:S(2)}) async-start(), calls=%async_computation.12 | async-start | bytes 5242880 | tf_op jit(solution)/shard_map/all_gather | solution.py:196
  26.8 112.1 %all-gather.15.cloned.1.call-start = ((), (), s32[]{:S(2)}) async-start(), calls=%async_computation.14 | async-start | bytes 2359296 | tf_op jit(solution)/shard_map/all_gather | solution.py:152
  27.5 205.5 %reduce-scatter.12.cloned.1.call-start = ((), (), s32[]{:S(2)}) async-start(), calls=%async_computation.15 | async-start | bytes 10485760 | tf_op jit(solution)/shard_map/reduce_scatter | solution.py:216
  146.5 170.0 %all-gather.17.cloned.1.call-start = ((), (), s32[]{:S(2)}) async-start(), calls=%async_computation.16 | async-start | bytes 9437184 | tf_op jit(solution)/shard_map/all_gather | solution.py:159
  147.1 251.4 %all-gather.19.cloned.1.call-start = ((), (), s32[]{:S(2)}) async-start(), calls=%async_computation.17 | async-start | bytes 9437184 | tf_op jit(solution)/shard_map/all_gather | solution.py:160
  147.7 333.4 %all-gather.21.cloned.1.call-start = ((), (), s32[]{:S(2)}) async-start(), calls=%async_computation.18 | async-start | bytes 9437184 | tf_op jit(solution)/shard_map/all_gather | solution.py:161
  160.2 599.6 %copy-start.31 = (f32[8,1,256]{2,1,0:T(1,128)}, f32[8,1,256]{2,1,0:T(1,128)S(1)}, u32[]{:S(2)}) copy-start(f32[8,1,256]{2,1,0:T(1,128)S(1)} %convert_element_type.105) | copy-start | bytes 24580
  236.5 523.4 %copy-start.8 = (f32[256,2048]{1,0:T(8,128)}, f32[256,2048]{1,0:T(8,128)S(1)}, u32[]{:S(2)}) copy-start(f32[256,2048]{1,0:T(8,128)S(1)} %get-tuple-element.215) | copy-start | bytes 6291460
  236.5 523.4 %copy-start.38 = (f32[256]{0:T(256)}, f32[256]{0:T(256)S(1)}, u32[]{:S(2)}) copy-start(f32[256]{0:T(256)S(1)} %add_rsqrt_fusion) | copy-start | bytes 3076
  239.4 77.1 %all-to-all-start = ((bf16[4,256,2048]{2,1,0:T(8,128)(2,1)}), bf16[4,256,2048]{2,1,0:T(8,128)(2,1)}, u32[]{:S(2)}, u32[]{:S(2)}) async-start(bf16[4,256,2048]{2,1,0:T(8,128)(2,1)} %stack.2), calls=%async_computation.1 | async-start | bytes 8388608 | tf_op jit(solution)/shard_map/all_to_all | solution.py:14
  244.4 290.0 %all-gather.23.cloned.1.call-start = ((), (), s32[]{:S(2)}) async-start(), calls=%async_computation.20 | async-start | bytes 5242880 | tf_op jit(solution)/shard_map/all_gather | solution.py:244
  245.1 425.5 %reduce-scatter.16.cloned.1.call-start = ((), (), s32[]{:S(2)}) async-start(), calls=%async_computation.21 | async-start | bytes 10485760 | tf_op jit(solution)/shard_map/reduce_scatter | solution.py:251
  584.1 175.7 %reduce-scatter.14.cloned.1.call-start = ((), (), s32[]{:S(2)}) async-start(), calls=%async_computation.19 | async-start | bytes 10485760 | tf_op jit(solution)/shard_map/reduce_scatter | solution.py:231
  598.7 161.2 %copy-start.12 = (bf16[256,2048]{1,0:T(8,128)(2,1)S(1)}, bf16[256,2048]{1,0:T(8,128)(2,1)}, u32[]{:S(2)}) copy-start(bf16[256,2048]{1,0:T(8,128)(2,1)} %param.27) | copy-start | bytes 3145732
  598.7 218.7 %all-gather.25.cloned.1.call-start = ((), (), s32[]{:S(2)}) async-start(), calls=%async_computation.22 | async-start | bytes 5242880 | tf_op jit(solution)/shard_map/all_gather | solution.py:271
  764.7 296.3 %reduce-scatter.18.cloned.1.call-start = ((), (), s32[]{:S(2)}) async-start(), calls=%async_computation.23 | async-start | bytes 10485760 | tf_op jit(solution)/shard_map/reduce_scatter | solution.py:291
  974.5 132.1 %reduce-scatter.22.cloned.1.call-start = ((), (), s32[]{:S(2)}) async-start(), calls=%async_computation.25 | async-start | bytes 1179648 | tf_op jit(solution)/shard_map/reduce_scatter | solution.py:306
  979.0 151.1 %reduce-scatter.24.cloned.1.call-start = ((), (), s32[]{:S(2)}) async-start(), calls=%async_computation.26 | async-start | bytes 1179648 | tf_op jit(solution)/shard_map/reduce_scatter | solution.py:307
  983.7 197.4 %reduce-scatter.20.cloned.1.call-start = ((), (), s32[]{:S(2)}) async-start(), calls=%async_computation.24 | async-start | bytes 4718592 | tf_op jit(solution)/shard_map/reduce_scatter | solution.py:305
  990.5 241.7 %reduce-scatter.26.cloned.1.call-start = ((), (), s32[]{:S(2)}) async-start(), calls=%async_computation.27 | async-start | bytes 4718592 | tf_op jit(solution)/shard_map/reduce_scatter | solution.py:308
  998.4 403.2 %reduce-scatter.28.cloned.1.call-start = ((), (), s32[]{:S(2)}) async-start(), calls=%async_computation.28 | async-start | bytes 18874368 | tf_op jit(solution)/shard_map/reduce_scatter | solution.py:263
  1013.9 557.2 %reduce-scatter.30.cloned.1.call-start = ((), (), s32[]{:S(2)}) async-start(), calls=%async_computation.29 | async-start | bytes 18874368 | tf_op jit(solution)/shard_map/reduce_scatter | solution.py:264
  1029.5 711.2 %reduce-scatter.32.cloned.1.call-start = ((), (), s32[]{:S(2)}) async-start(), calls=%async_computation.30 | async-start | bytes 18874368 | tf_op jit(solution)/shard_map/reduce_scatter | solution.py:265
  (59 other events, 1250.8 us)
Sparse Core Ops, SparseCore 0:
  9.6 36.1 all-gather.12
  48.3 51.8 all-gather.10
  101.7 30.5 all-gather.14
  146.7 86.3 reduce-scatter.11
  234.5 82.0 all-gather.16
  318.0 80.5 all-gather.18
  400.1 80.9 all-gather.20
  483.5 50.7 all-gather.22
  584.3 86.2 reduce-scatter.15
  673.5 86.3 reduce-scatter.13
  764.8 52.5 all-gather.24
  974.6 86.3 reduce-scatter.17
  1063.8 32.4 reduce-scatter.21
  1099.0 31.0 reduce-scatter.23
  1132.8 48.1 reduce-scatter.19
  1183.8 48.3 reduce-scatter.25
  1235.0 166.6 reduce-scatter.27
  1404.4 166.6 reduce-scatter.29
  1574.0 166.6 reduce-scatter.31
